TPU v7x, 32 devices: a whole 2x2x4 slice. The times are simulated.
32 devices in a mesh: dom: 8 (over z, y), sub: 4 (over x, core).
Axes of the slice: x: 2, y: 2, z: 4, core: 2. Of those that a mesh axis runs over, the one named last changes fastest.
Arguments:
- positions: float32 [2048, 3, 256], P(('dom', 'sub')), may hold values from -6 to 6
- time_bins: int32 [2048, 256], P(('dom', 'sub')), may hold values from 0 to 5
- home_groups: int32 [2048], P(('dom', 'sub')), may hold values from 0 to 63
- targets: int32 [2048, 4], P(('dom', 'sub')), may hold values from -1 to 7, as said below
- target_groups: int32 [2048, 4], P(('dom', 'sub')), may hold values from 0 to 63
- node_pos: float32 [3, 131072], P(None, ('dom', 'sub')), may hold values from -6 to 6
- node_mass: float32 [131072], P(('dom', 'sub')), may hold values from 0.2 to 2
- node_lists: int32 [512, 256], P('dom'), may hold values from 0 to 16383
- list_counts: int32 [512], P('dom'), may hold values from 64 to 256, as said below
Outputs:
- forces: float32 [2048, 3, 256], P(('dom', 'sub'))
Inputs may be any that keep to these rules, and one draw needn't show every extreme that they name: `targets`: row b names the remote domains that block b visits, each at most once and never its own domain b // 256; -1 marks an unused entry, in any column. The rows of one device name one domain at most 32 times, and some device names some domain exactly 32 times in every draw. The rows of one domain's 4 devices together name one domain at most 64 times, and this is reached in every draw. `list_counts`: each domain has at least one list with all 256 entries valid.
All inputs are finite; a program needn't handle non-finite values.
Results may differ from a plain program's by a relative error of at most 0.0003.
Values sent between devices are 32-bit elements; how exact they have to be, the bound alone decides.
A program may use at most 128 MiB of HBM per device.

v0:
```python
import jax
import jax.numpy as jnp
from jax import lax
from jax.sharding import PartitionSpec as P

CUR_BIN = 2
soften_sq = 0.04
gauss_slope = 1.1283791670955126


def prefix(part, axis, combine, identity):
    place = lax.axis_index(axis)
    gathered = lax.all_gather(part, axis)
    state = jnp.zeros_like(part) + jnp.asarray(identity, part.dtype)

    def one(step, state):
        return combine(state, lax.dynamic_index_in_dim(gathered, step, 0, False))

    return lax.fori_loop(0, place, one, state)


def short_pull(sink_pos, source_pos, source_mass):
    offset = sink_pos[:, None, :] - source_pos[:, :, None]
    range_sq = jnp.sum(offset * offset, axis=0) + soften_sq
    distance = jnp.sqrt(range_sq)
    scaled = distance * 0.5
    factor = lax.erfc(scaled) + gauss_slope * scaled * jnp.exp(-scaled * scaled)
    weight = source_mass[:, None] * factor / (range_sq * distance)
    return -jnp.sum(offset * weight[None, :, :], axis=1)


def list_tables(table_pos, table_mass, lists, counts):
    entry_ids = jnp.arange(lists.shape[1], dtype=jnp.int32)
    list_pos = jnp.transpose(table_pos[:, lists], (1, 0, 2))
    list_mass = table_mass[lists] * (entry_ids[None, :] < counts[:, None]).astype(jnp.float32)
    return (list_pos, list_mass)


def evaluate(sink_pos, list_rows, is_alive, list_pos, list_mass):
    item_count = sink_pos.shape[0]
    padded = -(-item_count // 8) * 8

    def one_item(sink_one, list_row, alive_one):
        return short_pull(sink_one, list_pos[list_row], list_mass[list_row] * alive_one)

    def one_group(operands):
        return jax.vmap(one_item)(*operands)

    width = sink_pos.shape[2]
    grouped = lax.map(
        one_group,
        (
            sink_pos.reshape(padded // 8, 8, 3, width),
            list_rows.reshape(padded // 8, 8),
            is_alive.reshape(padded // 8, 8),
        ),
    )
    return grouped.reshape(padded, 3, width)[:item_count]


def ranks_within(bucket, usable, bucket_count):
    onehot = (
        (bucket[:, None] == jnp.arange(bucket_count, dtype=jnp.int32)[None, :]) & usable[:, None]
    ).astype(jnp.int32)
    placed = jnp.sum((jnp.cumsum(onehot, axis=0) - onehot) * onehot, axis=1)
    return (placed, jnp.sum(onehot, axis=0))


def owners(slot_index, usable, slot_count):
    matches = (slot_index[None, :] == jnp.arange(slot_count, dtype=jnp.int32)[:, None]) & usable[
        None, :
    ]
    is_filled = jnp.any(matches, axis=1)
    source_row = jnp.sum(
        matches.astype(jnp.int32) * jnp.arange(slot_index.shape[0], dtype=jnp.int32)[None, :],
        axis=1,
    )
    return (source_row, is_filled)


def local(
    positions,
    time_bins,
    home_groups,
    targets,
    target_groups,
    node_pos,
    node_mass,
    node_lists,
    list_counts,
):
    domains = lax.axis_size("dom")
    sharers = lax.axis_size("sub")
    blocks, most_visits = targets.shape
    width = positions.shape[2]
    capacity = max(2, blocks * most_visits // domains)
    table_pos, table_mass = (
        lax.all_gather(node_pos, "sub", axis=1, tiled=True),
        lax.all_gather(node_mass, "sub", axis=0, tiled=True),
    )
    list_pos, list_mass = list_tables(table_pos, table_mass, node_lists, list_counts)
    home_force = evaluate(
        positions, home_groups, jnp.ones((blocks,), jnp.float32), list_pos, list_mass
    )
    flat_dest = targets.reshape(-1)
    usable = flat_dest >= 0
    safe_dest = jnp.maximum(flat_dest, 0)
    pair_block = jnp.arange(blocks * most_visits, dtype=jnp.int32) // most_visits
    flat_groups = target_groups.reshape(-1)
    within, per_domain = ranks_within(safe_dest, usable, domains)
    first_width = -(-capacity // sharers)
    second_width = -(-2 * capacity // sharers)
    offsets = prefix(
        per_domain, "sub", lambda earlier, later: earlier + later, jnp.zeros_like(per_domain)
    )
    row_place = offsets[safe_dest] + within
    sharer_of = row_place % sharers
    row_slot = row_place // sharers
    bucket = sharer_of * domains + safe_dest
    within_bucket, _ = ranks_within(bucket, usable, sharers * domains)
    first_slot = bucket * first_width + within_bucket
    source_row, is_filled = owners(first_slot, usable, sharers * domains * first_width)
    out_pos = jnp.where(is_filled[:, None, None], positions[pair_block[source_row]], 0.0).reshape(
        sharers, domains, first_width, 3, width
    )
    out_group = jnp.where(is_filled, flat_groups[source_row], -1).reshape(
        sharers, domains, first_width
    )
    out_slot = jnp.where(is_filled, row_slot[source_row], 0).reshape(sharers, domains, first_width)
    spread_pos, spread_group, spread_slot = (
        lax.all_to_all(out_pos, "sub", split_axis=0, concat_axis=0, tiled=True),
        lax.all_to_all(out_group, "sub", split_axis=0, concat_axis=0, tiled=True),
        lax.all_to_all(out_slot, "sub", split_axis=0, concat_axis=0, tiled=True),
    )
    arrival_dest = (
        jnp.arange(sharers * domains * first_width, dtype=jnp.int32) // first_width % domains
    )
    arrival_group = spread_group.reshape(-1)
    arrival_ok = arrival_group >= 0
    second_index = arrival_dest * second_width + spread_slot.reshape(-1)
    arrival_row, second_filled = owners(second_index, arrival_ok, domains * second_width)
    mid_pos = jnp.where(
        second_filled[:, None, None], spread_pos.reshape(-1, 3, width)[arrival_row], 0.0
    ).reshape(domains, second_width, 3, width)
    mid_group = jnp.where(second_filled, arrival_group[arrival_row], -1).reshape(
        domains, second_width
    )
    arrived_pos = lax.all_to_all(mid_pos, "dom", split_axis=0, concat_axis=0, tiled=True)
    arrived_group = lax.all_to_all(mid_group, "dom", split_axis=0, concat_axis=0, tiled=True)
    leading = arrived_group.shape
    flat_group = arrived_group.reshape(-1)
    pulled = evaluate(
        arrived_pos.reshape((-1, 3, width)),
        jnp.maximum(flat_group, 0),
        (flat_group >= 0).astype(jnp.float32),
        list_pos,
        list_mass,
    )
    computed = pulled.reshape(leading + (3, width))
    returned = lax.all_to_all(computed, "dom", split_axis=0, concat_axis=0, tiled=True)
    arrival_force = returned.reshape(domains * second_width, 3, width)[
        jnp.where(arrival_ok, second_index, 0)
    ]
    arrival_force = arrival_force * arrival_ok.astype(jnp.float32)[:, None, None]
    gathered_back = lax.all_to_all(
        arrival_force.reshape(sharers, domains, first_width, 3, width),
        "sub",
        split_axis=0,
        concat_axis=0,
        tiled=True,
    )
    pair_force = gathered_back.reshape(-1, 3, width)[jnp.where(usable, first_slot, 0)]
    pair_force = pair_force * usable.astype(jnp.float32)[:, None, None]
    remote = jnp.sum(pair_force.reshape(blocks, most_visits, 3, width), axis=1)
    active = (time_bins <= CUR_BIN).astype(jnp.float32)
    return (home_force + remote) * active[:, None, :]


def solution(mesh):
    return jax.shard_map(
        local,
        mesh=mesh,
        in_specs=(
            P(("dom", "sub"), None, None),
            P(("dom", "sub"), None),
            P(("dom", "sub")),
            P(("dom", "sub"), None),
            P(("dom", "sub"), None),
            P(None, ("dom", "sub")),
            P(("dom", "sub")),
            P("dom", None),
            P("dom"),
        ),
        out_specs=P(("dom", "sub"), None, None),
        check_vma=False,
    )
```

profile of v0, /device:TPU:0, one launch (start us, length us, event | category | flops | bytes accessed | tf_op | source)
XLA Modules:
  0.0 551.8 jit_solution(571146538005920362)
XLA Ops:
  5.3 6.4 %all-reduce.4 = s32[32]{0:T(128)S(1)} all-reduce(s32[32]{0:T(128)S(1)} %dynamic-update-slice), channel_id=2, replica_groups=mesh['dom'=8,'sub'=4] {'sub'}, use_global_device_ids=true, to_apply=%add.4 | all-reduce | flops 32 | bytes 256
  12.5 5.0 and_select_fusion.4
  18.7 1.9 gather_fusion.6
  21.6 1.9 gather_fusion.7
  24.4 3.2 all-to-all-start
  27.7 1.9 gather_fusion.8
  29.7 1.9 gather_fusion.9
  32.7 3.3 all-to-all-start.1
  36.0 3.7 all-to-all-done.1
  39.8 3.5 all-to-all-start.2
  45.7 9.2 %all-to-all-done.2 = f32[4,8,8,3,256]{4,2,1,3,0:T(8,128)S(1)} async-done(((f32[4,8,8,3,256]{4,2,1,3,0:T(8,128)}), f32[4,8,8,3,256]{4,2,1,3,0:T(8,128)S(1)}, u32[]{:S(2)}, u32[]{:S(2)}) %all-to-all-start.2) | async-done | bytes 786464 | tf_op jit(solution)/shard_map/all_to_all | solution.py:131
  54.9 5.8 %all-to-all-start.4 = ((s32[8,1,16]{2,1,0:T(1,128)}), s32[8,1,16]{2,1,0:T(1,128)S(1)}, u32[]{:S(2)}, u32[]{:S(2)}) async-start(s32[8,1,16]{2,1,0:T(1,128)} %bitcast.37), calls=%async_computation.4 | async-start | bytes 8192 | tf_op jit(solution)/shard_map/all_to_all | solution.py:149
  63.0 4.1 all-to-all-done.4
  67.1 3.5 all-to-all-start.3
  71.3 49.3 %all_gather.12 = f32[3,16384]{0,1:T(8,128)} all-gather(f32[3,4096]{0,1:T(8,128)S(1)} %copy.99), channel_id=1, replica_groups=mesh['dom'=8,'sub'=4] {'sub'}, dimensions={1}, use_global_device_ids=true | all-gather | bytes 245760 | tf_op jit(solution)/shard_map/all_gather | solution.py:98
  120.6 57.8 %gather_fusion.4 = f32[16384,3]{1,0:T(8,128)} fusion(f32[3,16384]{0,1:T(8,128)} %all_gather.12, s32[16384]{0:T(1024)S(1)} %broadcast_clamp_fusion), kind=kCustom, calls=%fused_computation.4 | custom fusion | bytes 458752 | tf_op jit(solution)/shard_map/gather | solution.py:34
  178.4 5.4 copy.100
  183.7 5.2 all_gather.13
  189.0 90.5 %gather_fusion.5 = f32[16384]{0:T(1024)S(1)} fusion(f32[16384]{0:T(1024)S(1)} %all_gather.13, s32[16384]{0:T(1024)S(1)} %broadcast_clamp_fusion), kind=kCustom, calls=%fused_computation.5 | custom fusion | bytes 196608 | tf_op jit(solution)/shard_map/gather | solution.py:35
  279.8 160.7 %while.36 = (s32[]{:T(128)}, f32[16,8,3,256]{3,2,1,0:T(4,128)}, f32[16,8,3,256]{3,1,0,2:T(8,128)S(1)}, s32[16,8]{1,0:T(8,128)S(1)}, f32[64,3,256]{2,1,0:T(4,128)...) while((s32[]{:T(128)}, f32[16,8,3,256]{3,2,1,0:T(4,128)}, ...), condition=%wide.region_20.21_spmd, body=%wide.region_17.20_spmd.sunk | while | flops 45615144 | bytes 8758177 | solution.py:50
  282.3 5.9 %fusion.90 = f32[8,256,256]{2,1,0:T(8,128)S(1)} fusion(f32[8,256,256]{2,1,0:T(8,128)S(1)} %fusion.88, f32[8,256]{1,0:T(8,128)S(1)} %broadcast_multiply_fusion.3), kind=kLoop, calls=%fused_computation.57.clone.1 | loop fusion | flops 36700160 | bytes 4202496 | tf_op jit(solution)/shard_map/while/body/eval_jaxpr/vmap()/div | solution.py:28
  292.4 5.9 %fusion.90 = f32[8,256,256]{2,1,0:T(8,128)S(1)} fusion(f32[8,256,256]{2,1,0:T(8,128)S(1)} %fusion.88, f32[8,256]{1,0:T(8,128)S(1)} %broadcast_multiply_fusion.3), kind=kLoop, calls=%fused_computation.57.clone.1 | loop fusion | flops 36700160 | bytes 4202496 | tf_op jit(solution)/shard_map/while/body/eval_jaxpr/vmap()/div | solution.py:28
  302.4 5.9 %fusion.90 = f32[8,256,256]{2,1,0:T(8,128)S(1)} fusion(f32[8,256,256]{2,1,0:T(8,128)S(1)} %fusion.88, f32[8,256]{1,0:T(8,128)S(1)} %broadcast_multiply_fusion.3), kind=kLoop, calls=%fused_computation.57.clone.1 | loop fusion | flops 36700160 | bytes 4202496 | tf_op jit(solution)/shard_map/while/body/eval_jaxpr/vmap()/div | solution.py:28
  312.4 5.9 %fusion.90 = f32[8,256,256]{2,1,0:T(8,128)S(1)} fusion(f32[8,256,256]{2,1,0:T(8,128)S(1)} %fusion.88, f32[8,256]{1,0:T(8,128)S(1)} %broadcast_multiply_fusion.3), kind=kLoop, calls=%fused_computation.57.clone.1 | loop fusion | flops 36700160 | bytes 4202496 | tf_op jit(solution)/shard_map/while/body/eval_jaxpr/vmap()/div | solution.py:28
  322.5 5.9 %fusion.90 = f32[8,256,256]{2,1,0:T(8,128)S(1)} fusion(f32[8,256,256]{2,1,0:T(8,128)S(1)} %fusion.88, f32[8,256]{1,0:T(8,128)S(1)} %broadcast_multiply_fusion.3), kind=kLoop, calls=%fused_computation.57.clone.1 | loop fusion | flops 36700160 | bytes 4202496 | tf_op jit(solution)/shard_map/while/body/eval_jaxpr/vmap()/div | solution.py:28
  332.5 5.9 %fusion.90 = f32[8,256,256]{2,1,0:T(8,128)S(1)} fusion(f32[8,256,256]{2,1,0:T(8,128)S(1)} %fusion.88, f32[8,256]{1,0:T(8,128)S(1)} %broadcast_multiply_fusion.3), kind=kLoop, calls=%fused_computation.57.clone.1 | loop fusion | flops 36700160 | bytes 4202496 | tf_op jit(solution)/shard_map/while/body/eval_jaxpr/vmap()/div | solution.py:28
  342.6 5.9 %fusion.90 = f32[8,256,256]{2,1,0:T(8,128)S(1)} fusion(f32[8,256,256]{2,1,0:T(8,128)S(1)} %fusion.88, f32[8,256]{1,0:T(8,128)S(1)} %broadcast_multiply_fusion.3), kind=kLoop, calls=%fused_computation.57.clone.1 | loop fusion | flops 36700160 | bytes 4202496 | tf_op jit(solution)/shard_map/while/body/eval_jaxpr/vmap()/div | solution.py:28
  352.6 5.9 %fusion.90 = f32[8,256,256]{2,1,0:T(8,128)S(1)} fusion(f32[8,256,256]{2,1,0:T(8,128)S(1)} %fusion.88, f32[8,256]{1,0:T(8,128)S(1)} %broadcast_multiply_fusion.3), kind=kLoop, calls=%fused_computation.57.clone.1 | loop fusion | flops 36700160 | bytes 4202496 | tf_op jit(solution)/shard_map/while/body/eval_jaxpr/vmap()/div | solution.py:28
  362.6 5.9 %fusion.90 = f32[8,256,256]{2,1,0:T(8,128)S(1)} fusion(f32[8,256,256]{2,1,0:T(8,128)S(1)} %fusion.88, f32[8,256]{1,0:T(8,128)S(1)} %broadcast_multiply_fusion.3), kind=kLoop, calls=%fused_computation.57.clone.1 | loop fusion | flops 36700160 | bytes 4202496 | tf_op jit(solution)/shard_map/while/body/eval_jaxpr/vmap()/div | solution.py:28
  372.7 5.9 %fusion.90 = f32[8,256,256]{2,1,0:T(8,128)S(1)} fusion(f32[8,256,256]{2,1,0:T(8,128)S(1)} %fusion.88, f32[8,256]{1,0:T(8,128)S(1)} %broadcast_multiply_fusion.3), kind=kLoop, calls=%fused_computation.57.clone.1 | loop fusion | flops 36700160 | bytes 4202496 | tf_op jit(solution)/shard_map/while/body/eval_jaxpr/vmap()/div | solution.py:28
  382.7 5.9 %fusion.90 = f32[8,256,256]{2,1,0:T(8,128)S(1)} fusion(f32[8,256,256]{2,1,0:T(8,128)S(1)} %fusion.88, f32[8,256]{1,0:T(8,128)S(1)} %broadcast_multiply_fusion.3), kind=kLoop, calls=%fused_computation.57.clone.1 | loop fusion | flops 36700160 | bytes 4202496 | tf_op jit(solution)/shard_map/while/body/eval_jaxpr/vmap()/div | solution.py:28
  392.8 5.9 %fusion.90 = f32[8,256,256]{2,1,0:T(8,128)S(1)} fusion(f32[8,256,256]{2,1,0:T(8,128)S(1)} %fusion.88, f32[8,256]{1,0:T(8,128)S(1)} %broadcast_multiply_fusion.3), kind=kLoop, calls=%fused_computation.57.clone.1 | loop fusion | flops 36700160 | bytes 4202496 | tf_op jit(solution)/shard_map/while/body/eval_jaxpr/vmap()/div | solution.py:28
  402.8 5.9 %fusion.90 = f32[8,256,256]{2,1,0:T(8,128)S(1)} fusion(f32[8,256,256]{2,1,0:T(8,128)S(1)} %fusion.88, f32[8,256]{1,0:T(8,128)S(1)} %broadcast_multiply_fusion.3), kind=kLoop, calls=%fused_computation.57.clone.1 | loop fusion | flops 36700160 | bytes 4202496 | tf_op jit(solution)/shard_map/while/body/eval_jaxpr/vmap()/div | solution.py:28
  412.9 5.9 %fusion.90 = f32[8,256,256]{2,1,0:T(8,128)S(1)} fusion(f32[8,256,256]{2,1,0:T(8,128)S(1)} %fusion.88, f32[8,256]{1,0:T(8,128)S(1)} %broadcast_multiply_fusion.3), kind=kLoop, calls=%fused_computation.57.clone.1 | loop fusion | flops 36700160 | bytes 4202496 | tf_op jit(solution)/shard_map/while/body/eval_jaxpr/vmap()/div | solution.py:28
  422.9 5.9 %fusion.90 = f32[8,256,256]{2,1,0:T(8,128)S(1)} fusion(f32[8,256,256]{2,1,0:T(8,128)S(1)} %fusion.88, f32[8,256]{1,0:T(8,128)S(1)} %broadcast_multiply_fusion.3), kind=kLoop, calls=%fused_computation.57.clone.1 | loop fusion | flops 36700160 | bytes 4202496 | tf_op jit(solution)/shard_map/while/body/eval_jaxpr/vmap()/div | solution.py:28
  432.9 5.9 %fusion.90 = f32[8,256,256]{2,1,0:T(8,128)S(1)} fusion(f32[8,256,256]{2,1,0:T(8,128)S(1)} %fusion.88, f32[8,256]{1,0:T(8,128)S(1)} %broadcast_multiply_fusion.3), kind=kLoop, calls=%fused_computation.57.clone.1 | loop fusion | flops 36700160 | bytes 4202496 | tf_op jit(solution)/shard_map/while/body/eval_jaxpr/vmap()/div | solution.py:28
  442.4 5.9 %all-to-all-start.5 = ((f32[8,16,3,256]{3,1,2,0:T(8,128)}), f32[8,16,3,256]{3,1,2,0:T(8,128)S(1)}, u32[]{:S(2)}, u32[]{:S(2)}) async-start(f32[8,16,3,256]{3,1,2,0:T(8,128)} %copy.114), calls=%async_computation.5 | async-start | bytes 786432 | tf_op jit(solution)/shard_map/all_to_all | solution.py:160
  448.8 11.7 %all-to-all-done.5 = f32[8,16,3,256]{3,1,2,0:T(8,128)S(1)} async-done(((f32[8,16,3,256]{3,1,2,0:T(8,128)}), f32[8,16,3,256]{3,1,2,0:T(8,128)S(1)}, u32[]{:S(2)}, u32[]{:S(2)}) %all-to-all-start.5) | async-done | bytes 393248 | tf_op jit(solution)/shard_map/all_to_all | solution.py:160
  463.3 3.5 all-to-all-start.6
  466.8 80.5 %while.34 = (s32[]{:T(128)}, f32[8,8,3,256]{3,2,1,0:T(4,128)}, f32[8,8,3,256]{3,2,1,0:T(4,128)S(1)}, s32[8,8]{1,0:T(8,128)S(1)}, f32[64,3,256]{2,1,0:T(4,128)S(1)}, /*index=5*/f32[64,256]{1,0:T(8,128)S(1)}, s32[]{:T(128)}) while((s32[]{:T(128)}, f32[8,8,3,256]{3,2,1,0:T(4,128)}, f32[8,8,3,256]{3,2,1,0:T(4,128)S(1)}, s32[8,8]{1,0:T(8,128)S(1)}, ...), condition=%wide.region_3.4_spmd, body=%wide.region_0.3_spmd.sunk | while | flops 45613096 | bytes 10265453 | solution.py:50
  469.3 5.9 %fusion.86 = f32[8,256,256]{2,1,0:T(8,128)S(1)} fusion(f32[8,256,256]{2,1,0:T(8,128)S(1)} %fusion.85, f32[8,256]{1,0:T(8,128)S(1)} %gather_fusion.1), kind=kLoop, calls=%fused_computation.27.clone.1 | loop fusion | flops 36700160 | bytes 4202496 | tf_op jit(solution)/shard_map/while/body/eval_jaxpr/vmap()/div | solution.py:28
  479.3 5.9 %fusion.86 = f32[8,256,256]{2,1,0:T(8,128)S(1)} fusion(f32[8,256,256]{2,1,0:T(8,128)S(1)} %fusion.85, f32[8,256]{1,0:T(8,128)S(1)} %gather_fusion.1), kind=kLoop, calls=%fused_computation.27.clone.1 | loop fusion | flops 36700160 | bytes 4202496 | tf_op jit(solution)/shard_map/while/body/eval_jaxpr/vmap()/div | solution.py:28
  489.4 5.9 %fusion.86 = f32[8,256,256]{2,1,0:T(8,128)S(1)} fusion(f32[8,256,256]{2,1,0:T(8,128)S(1)} %fusion.85, f32[8,256]{1,0:T(8,128)S(1)} %gather_fusion.1), kind=kLoop, calls=%fused_computation.27.clone.1 | loop fusion | flops 36700160 | bytes 4202496 | tf_op jit(solution)/shard_map/while/body/eval_jaxpr/vmap()/div | solution.py:28
  499.4 5.9 %fusion.86 = f32[8,256,256]{2,1,0:T(8,128)S(1)} fusion(f32[8,256,256]{2,1,0:T(8,128)S(1)} %fusion.85, f32[8,256]{1,0:T(8,128)S(1)} %gather_fusion.1), kind=kLoop, calls=%fused_computation.27.clone.1 | loop fusion | flops 36700160 | bytes 4202496 | tf_op jit(solution)/shard_map/while/body/eval_jaxpr/vmap()/div | solution.py:28
  509.5 5.9 %fusion.86 = f32[8,256,256]{2,1,0:T(8,128)S(1)} fusion(f32[8,256,256]{2,1,0:T(8,128)S(1)} %fusion.85, f32[8,256]{1,0:T(8,128)S(1)} %gather_fusion.1), kind=kLoop, calls=%fused_computation.27.clone.1 | loop fusion | flops 36700160 | bytes 4202496 | tf_op jit(solution)/shard_map/while/body/eval_jaxpr/vmap()/div | solution.py:28
  519.5 5.9 %fusion.86 = f32[8,256,256]{2,1,0:T(8,128)S(1)} fusion(f32[8,256,256]{2,1,0:T(8,128)S(1)} %fusion.85, f32[8,256]{1,0:T(8,128)S(1)} %gather_fusion.1), kind=kLoop, calls=%fused_computation.27.clone.1 | loop fusion | flops 36700160 | bytes 4202496 | tf_op jit(solution)/shard_map/while/body/eval_jaxpr/vmap()/div | solution.py:28
  529.6 5.9 %fusion.86 = f32[8,256,256]{2,1,0:T(8,128)S(1)} fusion(f32[8,256,256]{2,1,0:T(8,128)S(1)} %fusion.85, f32[8,256]{1,0:T(8,128)S(1)} %gather_fusion.1), kind=kLoop, calls=%fused_computation.27.clone.1 | loop fusion | flops 36700160 | bytes 4202496 | tf_op jit(solution)/shard_map/while/body/eval_jaxpr/vmap()/div | solution.py:28
  539.7 5.9 %fusion.86 = f32[8,256,256]{2,1,0:T(8,128)S(1)} fusion(f32[8,256,256]{2,1,0:T(8,128)S(1)} %fusion.85, f32[8,256]{1,0:T(8,128)S(1)} %gather_fusion.1), kind=kLoop, calls=%fused_computation.27.clone.1 | loop fusion | flops 36700160 | bytes 4202496 | tf_op jit(solution)/shard_map/while/body/eval_jaxpr/vmap()/div | solution.py:28
  (363 shorter events, 123.3 us)
Async XLA Ops:
  0.0 29.6 %copy-start = (f32[64,3,256]{2,0,1:T(8,128)S(1)}, f32[64,3,256]{2,0,1:T(8,128)}, u32[]{:S(2)}) copy-start(f32[64,3,256]{2,0,1:T(8,128)} %param.15) | copy-start | bytes 589828
  24.4 8.3 %all-to-all-start = ((s32[4,8,8]{2,1,0:T(8,128)}), s32[4,8,8]{2,1,0:T(8,128)S(1)}, u32[]{:S(2)}, u32[]{:S(2)}) async-start(s32[4,8,8]{2,1,0:T(8,128)} %get-tuple-element.261), calls=%async_computation | async-start | bytes 32768 | tf_op jit(solution)/shard_map/all_to_all | solution.py:133
  29.6 3.0 copy-start.4
  32.7 7.1 %all-to-all-start.1 = ((s32[4,8,8]{2,1,0:T(8,128)}), s32[4,8,8]{2,1,0:T(8,128)S(1)}, u32[]{:S(2)}, u32[]{:S(2)}) async-start(s32[4,8,8]{2,1,0:T(8,128)} %get-tuple-element.260), calls=%async_computation.1 | async-start | bytes 32768 | tf_op jit(solution)/shard_map/all_to_all | solution.py:132
  39.8 15.1 %all-to-all-start.2 = ((f32[4,8,8,3,256]{4,2,1,3,0:T(8,128)}), f32[4,8,8,3,256]{4,2,1,3,0:T(8,128)S(1)}, u32[]{:S(2)}, u32[]{:S(2)}) async-start(f32[4,8,8,3,256]{4,2,1,3,0:T(8,128)} %copy_select_fusion), calls=%async_computation.2 | async-start | bytes 1572864 | tf_op jit(solution)/shard_map/all_to_all | solution.py:131
  54.9 12.3 %all-to-all-start.4 = ((s32[8,1,16]{2,1,0:T(1,128)}), s32[8,1,16]{2,1,0:T(1,128)S(1)}, u32[]{:S(2)}, u32[]{:S(2)}) async-start(s32[8,1,16]{2,1,0:T(1,128)} %bitcast.37), calls=%async_computation.4 | async-start | bytes 8192 | tf_op jit(solution)/shard_map/all_to_all | solution.py:149
  60.7 9.9 %copy-start.3 = (f32[3,4096]{1,0:T(4,128)S(1)}, f32[3,4096]{1,0:T(4,128)}, u32[]{:S(2)}) copy-start(f32[3,4096]{1,0:T(4,128)} %param.20) | copy-start | bytes 147460
  67.1 212.7 %all-to-all-start.3 = ((f32[8,16,3,256]{3,1,2,0:T(8,128)}), f32[8,16,3,256]{3,1,2,0:T(8,128)S(1)}, u32[]{:S(2)}, u32[]{:S(2)}) async-start(f32[8,16,3,256]{3,1,2,0:T(8,128)} %copy_select_fusion.1), calls=%async_computation.3 | async-start | bytes 786432 | tf_op jit(solution)/shard_map/all_to_all | solution.py:148
  178.4 5.4 copy-start.6
  189.0 90.6 %copy-start.7 = (s32[64]{0:T(128)S(1)}, s32[64]{0:T(128)}, u32[]{:S(2)}) copy-start(s32[64]{0:T(128)} %param.23) | copy-start | bytes 772
  440.5 7.9 %copy-start.8 = (s32[64]{0:T(128)S(1)}, s32[64]{0:T(128)}, u32[]{:S(2)}) copy-start(s32[64]{0:T(128)} %param.17) | copy-start | bytes 772
  442.4 18.1 %all-to-all-start.5 = ((f32[8,16,3,256]{3,1,2,0:T(8,128)}), f32[8,16,3,256]{3,1,2,0:T(8,128)S(1)}, u32[]{:S(2)}, u32[]{:S(2)}) async-start(f32[8,16,3,256]{3,1,2,0:T(8,128)} %copy.114), calls=%async_computation.5 | async-start | bytes 786432 | tf_op jit(solution)/shard_map/all_to_all | solution.py:160
  463.3 84.4 %all-to-all-start.6 = ((f32[4,8,8,3,256]{4,2,3,1,0:T(8,128)}), f32[4,8,8,3,256]{4,2,3,1,0:T(8,128)S(1)}, u32[]{:S(2)}, u32[]{:S(2)}) async-start(f32[4,8,8,3,256]{4,2,3,1,0:T(8,128)} %copy.118), calls=%async_computation.6 | async-start | bytes 1572864 | tf_op jit(solution)/shard_map/all_to_all | solution.py:165
  466.8 80.8 %copy-start.5 = (s32[64,256]{1,0:T(8,128)S(1)}, s32[64,256]{1,0:T(8,128)}, u32[]{:S(2)}) copy-start(s32[64,256]{1,0:T(8,128)} %param.16) | copy-start | bytes 196612
  466.8 0.7 copy-start.1
  475.2 1.7 copy-start.2
  476.9 0.7 copy-start.1
  485.2 1.7 copy-start.2
  486.9 0.7 copy-start.1
  495.3 1.7 copy-start.2
  497.0 0.7 copy-start.1
  505.3 1.7 copy-start.2
  507.1 0.7 copy-start.1
  515.4 1.7 copy-start.2
  517.1 0.7 copy-start.1
  525.4 1.7 copy-start.2
  527.2 0.7 copy-start.1
  535.5 1.7 copy-start.2
  537.2 0.7 copy-start.1
  545.6 1.7 copy-start.2
where the time goes:
time: 553 us; the launch traced here: 552 us
  other arithmetic  223 us (40%)
  local copies, waits for them, and re-layouts  208 us (38%)
  blocking collectives  60.9 us (11%)
  starting transfers between devices  28.7 us (5%)
  waiting for transfers between devices  28.7 us (5%)
    div x24, other arithmetic, short_pull(): weight = source_mass[:, None] * factor / (range_sq * distance)  141 us
    gather x2, local copies, waits for them, and re-layouts, list_tables(): table_mass[lists]  90.5 us
    gather x2, local copies, waits for them, and re-layouts, list_tables(): list_pos = jnp.transpose(table_pos[:, lists], (1, 0, 2))  63.1 us
    all_gather x1, blocking collectives, local(): lax.all_gather(node_pos, 'sub', axis=1, tiled=True)  49.3 us
    reduce_sum x24, other arithmetic, short_pull(): range_sq = jnp.sum(offset * offset, axis=0) + soften_sq  26.5 us
    reduce_sum x24, other arithmetic, short_pull(): return -jnp.sum(offset * weight[None, :, :], axis=1)  26.1 us
    dynamic_update_slice x24, other arithmetic, evaluate(): lax.map(one_group, (sink_pos.reshape(padded // 8, 8, 3, width), list_rows...  14.8 us
    gather x24, local copies, waits for them, and re-layouts, one_item(): list_pos[list_row]  14.4 us
  transfers between devices with their start and end apart: 7, of which 4 were waited for; matrix products, arithmetic and copies ran while one was open for 44% of the time, Pallas kernels for 0%

commit v1 on v0

--- a/solution.py
+++ b/solution.py
@@ -95,7 +95,7 @@
     width = positions.shape[2]
     capacity = max(2, blocks * most_visits // domains)
     table_pos, table_mass = (
-        lax.all_gather(node_pos, "sub", axis=1, tiled=True),
+        jnp.concatenate(lax.all_gather(node_pos, "sub"), axis=1),
         lax.all_gather(node_mass, "sub", axis=0, tiled=True),
     )
     list_pos, list_mass = list_tables(table_pos, table_mass, node_lists, list_counts)

time: 553 us -> 513 us (0.928)
  blocking collectives: 60.9 us -> 17.6 us
    all_gather x1, blocking collectives: 49.3 us -> 5.78 us  [local(): lax.all_gather(node_pos, 'sub')]
  transfers between devices with their start and end apart: 7 -> 7, of which waited for: 4 -> 4; matrix products, arithmetic and copies ran while one was open for 44% -> 48% of each run, Pallas kernels for 0% -> 0%
where the time goes in v1:
time: 513 us
  other arithmetic  223 us (43%)
  local copies, waits for them, and re-layouts  212 us (41%)
  starting transfers between devices  28.7 us (6%)
  waiting for transfers between devices  28.7 us (6%)
  blocking collectives  17.6 us (3%)
    div x24, other arithmetic, short_pull(): weight = source_mass[:, None] * factor / (range_sq * distance)  141 us
    gather x2, local copies, waits for them, and re-layouts, list_tables(): table_mass[lists]  90.5 us
    gather x2, local copies, waits for them, and re-layouts, list_tables(): list_pos = jnp.transpose(table_pos[:, lists], (1, 0, 2))  63.1 us
    reduce_sum x24, other arithmetic, short_pull(): range_sq = jnp.sum(offset * offset, axis=0) + soften_sq  26.5 us
    reduce_sum x24, other arithmetic, short_pull(): return -jnp.sum(offset * weight[None, :, :], axis=1)  26.1 us
    dynamic_update_slice x24, other arithmetic, evaluate(): lax.map(one_group, (sink_pos.reshape(padded // 8, 8, 3, width), list_rows...  14.8 us
    gather x24, local copies, waits for them, and re-layouts, one_item(): list_pos[list_row]  14.4 us
    gather x24, local copies, waits for them, and re-layouts, one_item(): list_mass[list_row] * alive_one  14 us
  transfers between devices with their start and end apart: 7, of which 4 were waited for; matrix products, arithmetic and copies ran while one was open for 48% of the time, Pallas kernels for 0%

profile of v1, /device:TPU:0, one launch (start us, length us, event | category | flops | bytes accessed | tf_op | source)
XLA Modules:
  0.0 512.6 jit_solution(11440188210197270234)
XLA Ops:
  5.3 6.4 %all-reduce.4 = s32[32]{0:T(128)S(1)} all-reduce(s32[32]{0:T(128)S(1)} %dynamic-update-slice), channel_id=3, replica_groups=mesh['dom'=8,'sub'=4] {'sub'}, use_global_device_ids=true, to_apply=%add.4 | all-reduce | flops 32 | bytes 256
  12.5 5.0 and_select_fusion.4
  18.7 1.9 gather_fusion.6
  21.6 1.9 gather_fusion.7
  24.4 3.2 all-to-all-start
  27.7 1.9 gather_fusion.8
  32.7 3.3 all-to-all-start.1
  36.0 3.7 all-to-all-done.1
  39.8 3.5 all-to-all-start.2
  45.7 9.2 %all-to-all-done.2 = f32[4,8,8,3,256]{4,2,1,3,0:T(8,128)S(1)} async-done(((f32[4,8,8,3,256]{4,2,1,3,0:T(8,128)}), f32[4,8,8,3,256]{4,2,1,3,0:T(8,128)S(1)}, u32[]{:S(2)}, u32[]{:S(2)}) %all-to-all-start.2) | async-done | bytes 786464 | tf_op jit(solution)/shard_map/all_to_all | solution.py:131
  54.9 5.8 %all-to-all-start.4 = ((s32[8,1,16]{2,1,0:T(1,128)}), s32[8,1,16]{2,1,0:T(1,128)S(1)}, u32[]{:S(2)}, u32[]{:S(2)}) async-start(s32[8,1,16]{2,1,0:T(1,128)} %bitcast.40), calls=%async_computation.4 | async-start | bytes 8192 | tf_op jit(solution)/shard_map/all_to_all | solution.py:149
  63.0 4.1 all-to-all-done.4
  67.1 3.5 all-to-all-start.3
  70.6 5.8 %all-gather.2 = f32[4,3,4096]{2,1,0:T(4,128)S(1)} all-gather(f32[1,3,4096]{2,1,0:T(4,128)S(1)} %bitcast.134), channel_id=2, replica_groups=mesh['dom'=8,'sub'=4] {'sub'}, dimensions={0}, use_global_device_ids=true | all-gather | bytes 245760 | tf_op jit(solution)/shard_map/all_gather | solution.py:98
  76.4 4.8 copy.99
  81.2 57.8 %gather_fusion.4 = f32[16384,3]{1,0:T(8,128)} fusion(f32[3,16384]{0,1:T(8,128)} %bitcast.119, s32[16384]{0:T(1024)S(1)} %broadcast_clamp_fusion), kind=kCustom, calls=%fused_computation.4 | custom fusion | bytes 458752 | tf_op jit(solution)/shard_map/gather | solution.py:34
  139.0 5.4 %copy.100 = f32[64,256,3]{1,2,0:T(4,128)S(1)} copy(f32[64,256,3]{2,1,0:T(8,128)} %bitcast.120) | data formatting | bytes 393216 | tf_op jit(solution)/shard_map/gather | solution.py:34
  144.3 5.4 %all_gather.17 = f32[16384]{0:T(1024)S(1)} all-gather(f32[4096]{0:T(1024)S(1)} %copy-done.6), channel_id=1, replica_groups=mesh['dom'=8,'sub'=4] {'sub'}, dimensions={0}, use_global_device_ids=true | all-gather | bytes 81920 | tf_op jit(solution)/shard_map/all_gather | solution.py:99
  149.8 90.5 %gather_fusion.5 = f32[16384]{0:T(1024)S(1)} fusion(f32[16384]{0:T(1024)S(1)} %all_gather.17, s32[16384]{0:T(1024)S(1)} %broadcast_clamp_fusion), kind=kCustom, calls=%fused_computation.5 | custom fusion | bytes 196608 | tf_op jit(solution)/shard_map/gather | solution.py:35
  240.6 160.7 %while.36 = (s32[]{:T(128)}, f32[16,8,3,256]{3,2,1,0:T(4,128)}, f32[16,8,3,256]{3,1,0,2:T(8,128)S(1)}, s32[16,8]{1,0:T(8,128)S(1)}, f32[64,3,256]{2,1,0:T(4,128)...) while((s32[]{:T(128)}, f32[16,8,3,256]{3,2,1,0:T(4,128)}, ...), condition=%wide.region_20.21_spmd, body=%wide.region_17.20_spmd.sunk | while | flops 45615144 | bytes 8758177 | solution.py:50
  243.1 5.9 %fusion.90 = f32[8,256,256]{2,1,0:T(8,128)S(1)} fusion(f32[8,256,256]{2,1,0:T(8,128)S(1)} %fusion.88, f32[8,256]{1,0:T(8,128)S(1)} %broadcast_multiply_fusion.3), kind=kLoop, calls=%fused_computation.57.clone.1 | loop fusion | flops 36700160 | bytes 4202496 | tf_op jit(solution)/shard_map/while/body/eval_jaxpr/vmap()/div | solution.py:28
  253.1 5.9 %fusion.90 = f32[8,256,256]{2,1,0:T(8,128)S(1)} fusion(f32[8,256,256]{2,1,0:T(8,128)S(1)} %fusion.88, f32[8,256]{1,0:T(8,128)S(1)} %broadcast_multiply_fusion.3), kind=kLoop, calls=%fused_computation.57.clone.1 | loop fusion | flops 36700160 | bytes 4202496 | tf_op jit(solution)/shard_map/while/body/eval_jaxpr/vmap()/div | solution.py:28
  263.2 5.9 %fusion.90 = f32[8,256,256]{2,1,0:T(8,128)S(1)} fusion(f32[8,256,256]{2,1,0:T(8,128)S(1)} %fusion.88, f32[8,256]{1,0:T(8,128)S(1)} %broadcast_multiply_fusion.3), kind=kLoop, calls=%fused_computation.57.clone.1 | loop fusion | flops 36700160 | bytes 4202496 | tf_op jit(solution)/shard_map/while/body/eval_jaxpr/vmap()/div | solution.py:28
  273.2 5.9 %fusion.90 = f32[8,256,256]{2,1,0:T(8,128)S(1)} fusion(f32[8,256,256]{2,1,0:T(8,128)S(1)} %fusion.88, f32[8,256]{1,0:T(8,128)S(1)} %broadcast_multiply_fusion.3), kind=kLoop, calls=%fused_computation.57.clone.1 | loop fusion | flops 36700160 | bytes 4202496 | tf_op jit(solution)/shard_map/while/body/eval_jaxpr/vmap()/div | solution.py:28
  283.3 5.9 %fusion.90 = f32[8,256,256]{2,1,0:T(8,128)S(1)} fusion(f32[8,256,256]{2,1,0:T(8,128)S(1)} %fusion.88, f32[8,256]{1,0:T(8,128)S(1)} %broadcast_multiply_fusion.3), kind=kLoop, calls=%fused_computation.57.clone.1 | loop fusion | flops 36700160 | bytes 4202496 | tf_op jit(solution)/shard_map/while/body/eval_jaxpr/vmap()/div | solution.py:28
  293.3 5.9 %fusion.90 = f32[8,256,256]{2,1,0:T(8,128)S(1)} fusion(f32[8,256,256]{2,1,0:T(8,128)S(1)} %fusion.88, f32[8,256]{1,0:T(8,128)S(1)} %broadcast_multiply_fusion.3), kind=kLoop, calls=%fused_computation.57.clone.1 | loop fusion | flops 36700160 | bytes 4202496 | tf_op jit(solution)/shard_map/while/body/eval_jaxpr/vmap()/div | solution.py:28
  303.4 5.9 %fusion.90 = f32[8,256,256]{2,1,0:T(8,128)S(1)} fusion(f32[8,256,256]{2,1,0:T(8,128)S(1)} %fusion.88, f32[8,256]{1,0:T(8,128)S(1)} %broadcast_multiply_fusion.3), kind=kLoop, calls=%fused_computation.57.clone.1 | loop fusion | flops 36700160 | bytes 4202496 | tf_op jit(solution)/shard_map/while/body/eval_jaxpr/vmap()/div | solution.py:28
  313.4 5.9 %fusion.90 = f32[8,256,256]{2,1,0:T(8,128)S(1)} fusion(f32[8,256,256]{2,1,0:T(8,128)S(1)} %fusion.88, f32[8,256]{1,0:T(8,128)S(1)} %broadcast_multiply_fusion.3), kind=kLoop, calls=%fused_computation.57.clone.1 | loop fusion | flops 36700160 | bytes 4202496 | tf_op jit(solution)/shard_map/while/body/eval_jaxpr/vmap()/div | solution.py:28
  323.4 5.9 %fusion.90 = f32[8,256,256]{2,1,0:T(8,128)S(1)} fusion(f32[8,256,256]{2,1,0:T(8,128)S(1)} %fusion.88, f32[8,256]{1,0:T(8,128)S(1)} %broadcast_multiply_fusion.3), kind=kLoop, calls=%fused_computation.57.clone.1 | loop fusion | flops 36700160 | bytes 4202496 | tf_op jit(solution)/shard_map/while/body/eval_jaxpr/vmap()/div | solution.py:28
  333.5 5.9 %fusion.90 = f32[8,256,256]{2,1,0:T(8,128)S(1)} fusion(f32[8,256,256]{2,1,0:T(8,128)S(1)} %fusion.88, f32[8,256]{1,0:T(8,128)S(1)} %broadcast_multiply_fusion.3), kind=kLoop, calls=%fused_computation.57.clone.1 | loop fusion | flops 36700160 | bytes 4202496 | tf_op jit(solution)/shard_map/while/body/eval_jaxpr/vmap()/div | solution.py:28
  343.5 5.9 %fusion.90 = f32[8,256,256]{2,1,0:T(8,128)S(1)} fusion(f32[8,256,256]{2,1,0:T(8,128)S(1)} %fusion.88, f32[8,256]{1,0:T(8,128)S(1)} %broadcast_multiply_fusion.3), kind=kLoop, calls=%fused_computation.57.clone.1 | loop fusion | flops 36700160 | bytes 4202496 | tf_op jit(solution)/shard_map/while/body/eval_jaxpr/vmap()/div | solution.py:28
  353.6 5.9 %fusion.90 = f32[8,256,256]{2,1,0:T(8,128)S(1)} fusion(f32[8,256,256]{2,1,0:T(8,128)S(1)} %fusion.88, f32[8,256]{1,0:T(8,128)S(1)} %broadcast_multiply_fusion.3), kind=kLoop, calls=%fused_computation.57.clone.1 | loop fusion | flops 36700160 | bytes 4202496 | tf_op jit(solution)/shard_map/while/body/eval_jaxpr/vmap()/div | solution.py:28
  363.6 5.9 %fusion.90 = f32[8,256,256]{2,1,0:T(8,128)S(1)} fusion(f32[8,256,256]{2,1,0:T(8,128)S(1)} %fusion.88, f32[8,256]{1,0:T(8,128)S(1)} %broadcast_multiply_fusion.3), kind=kLoop, calls=%fused_computation.57.clone.1 | loop fusion | flops 36700160 | bytes 4202496 | tf_op jit(solution)/shard_map/while/body/eval_jaxpr/vmap()/div | solution.py:28
  373.7 5.9 %fusion.90 = f32[8,256,256]{2,1,0:T(8,128)S(1)} fusion(f32[8,256,256]{2,1,0:T(8,128)S(1)} %fusion.88, f32[8,256]{1,0:T(8,128)S(1)} %broadcast_multiply_fusion.3), kind=kLoop, calls=%fused_computation.57.clone.1 | loop fusion | flops 36700160 | bytes 4202496 | tf_op jit(solution)/shard_map/while/body/eval_jaxpr/vmap()/div | solution.py:28
  383.7 5.9 %fusion.90 = f32[8,256,256]{2,1,0:T(8,128)S(1)} fusion(f32[8,256,256]{2,1,0:T(8,128)S(1)} %fusion.88, f32[8,256]{1,0:T(8,128)S(1)} %broadcast_multiply_fusion.3), kind=kLoop, calls=%fused_computation.57.clone.1 | loop fusion | flops 36700160 | bytes 4202496 | tf_op jit(solution)/shard_map/while/body/eval_jaxpr/vmap()/div | solution.py:28
  393.7 5.9 %fusion.90 = f32[8,256,256]{2,1,0:T(8,128)S(1)} fusion(f32[8,256,256]{2,1,0:T(8,128)S(1)} %fusion.88, f32[8,256]{1,0:T(8,128)S(1)} %broadcast_multiply_fusion.3), kind=kLoop, calls=%fused_computation.57.clone.1 | loop fusion | flops 36700160 | bytes 4202496 | tf_op jit(solution)/shard_map/while/body/eval_jaxpr/vmap()/div | solution.py:28
  403.2 5.9 %all-to-all-start.5 = ((f32[8,16,3,256]{3,1,2,0:T(8,128)}), f32[8,16,3,256]{3,1,2,0:T(8,128)S(1)}, u32[]{:S(2)}, u32[]{:S(2)}) async-start(f32[8,16,3,256]{3,1,2,0:T(8,128)} %copy.114), calls=%async_computation.5 | async-start | bytes 786432 | tf_op jit(solution)/shard_map/all_to_all | solution.py:160
  409.6 11.7 %all-to-all-done.5 = f32[8,16,3,256]{3,1,2,0:T(8,128)S(1)} async-done(((f32[8,16,3,256]{3,1,2,0:T(8,128)}), f32[8,16,3,256]{3,1,2,0:T(8,128)S(1)}, u32[]{:S(2)}, u32[]{:S(2)}) %all-to-all-start.5) | async-done | bytes 393248 | tf_op jit(solution)/shard_map/all_to_all | solution.py:160
  424.1 3.5 all-to-all-start.6
  427.6 80.5 %while.34 = (s32[]{:T(128)}, f32[8,8,3,256]{3,2,1,0:T(4,128)}, f32[8,8,3,256]{3,2,1,0:T(4,128)S(1)}, s32[8,8]{1,0:T(8,128)S(1)}, f32[64,3,256]{2,1,0:T(4,128)S(1)}, /*index=5*/f32[64,256]{1,0:T(8,128)S(1)}, s32[]{:T(128)}) while((s32[]{:T(128)}, f32[8,8,3,256]{3,2,1,0:T(4,128)}, f32[8,8,3,256]{3,2,1,0:T(4,128)S(1)}, s32[8,8]{1,0:T(8,128)S(1)}, ...), condition=%wide.region_3.4_spmd, body=%wide.region_0.3_spmd.sunk | while | flops 45613096 | bytes 10265453 | solution.py:50
  430.1 5.9 %fusion.86 = f32[8,256,256]{2,1,0:T(8,128)S(1)} fusion(f32[8,256,256]{2,1,0:T(8,128)S(1)} %fusion.85, f32[8,256]{1,0:T(8,128)S(1)} %gather_fusion.1), kind=kLoop, calls=%fused_computation.27.clone.1 | loop fusion | flops 36700160 | bytes 4202496 | tf_op jit(solution)/shard_map/while/body/eval_jaxpr/vmap()/div | solution.py:28
  440.1 5.9 %fusion.86 = f32[8,256,256]{2,1,0:T(8,128)S(1)} fusion(f32[8,256,256]{2,1,0:T(8,128)S(1)} %fusion.85, f32[8,256]{1,0:T(8,128)S(1)} %gather_fusion.1), kind=kLoop, calls=%fused_computation.27.clone.1 | loop fusion | flops 36700160 | bytes 4202496 | tf_op jit(solution)/shard_map/while/body/eval_jaxpr/vmap()/div | solution.py:28
  450.2 5.9 %fusion.86 = f32[8,256,256]{2,1,0:T(8,128)S(1)} fusion(f32[8,256,256]{2,1,0:T(8,128)S(1)} %fusion.85, f32[8,256]{1,0:T(8,128)S(1)} %gather_fusion.1), kind=kLoop, calls=%fused_computation.27.clone.1 | loop fusion | flops 36700160 | bytes 4202496 | tf_op jit(solution)/shard_map/while/body/eval_jaxpr/vmap()/div | solution.py:28
  460.2 5.9 %fusion.86 = f32[8,256,256]{2,1,0:T(8,128)S(1)} fusion(f32[8,256,256]{2,1,0:T(8,128)S(1)} %fusion.85, f32[8,256]{1,0:T(8,128)S(1)} %gather_fusion.1), kind=kLoop, calls=%fused_computation.27.clone.1 | loop fusion | flops 36700160 | bytes 4202496 | tf_op jit(solution)/shard_map/while/body/eval_jaxpr/vmap()/div | solution.py:28
  470.3 5.9 %fusion.86 = f32[8,256,256]{2,1,0:T(8,128)S(1)} fusion(f32[8,256,256]{2,1,0:T(8,128)S(1)} %fusion.85, f32[8,256]{1,0:T(8,128)S(1)} %gather_fusion.1), kind=kLoop, calls=%fused_computation.27.clone.1 | loop fusion | flops 36700160 | bytes 4202496 | tf_op jit(solution)/shard_map/while/body/eval_jaxpr/vmap()/div | solution.py:28
  480.3 5.9 %fusion.86 = f32[8,256,256]{2,1,0:T(8,128)S(1)} fusion(f32[8,256,256]{2,1,0:T(8,128)S(1)} %fusion.85, f32[8,256]{1,0:T(8,128)S(1)} %gather_fusion.1), kind=kLoop, calls=%fused_computation.27.clone.1 | loop fusion | flops 36700160 | bytes 4202496 | tf_op jit(solution)/shard_map/while/body/eval_jaxpr/vmap()/div | solution.py:28
  490.4 5.9 %fusion.86 = f32[8,256,256]{2,1,0:T(8,128)S(1)} fusion(f32[8,256,256]{2,1,0:T(8,128)S(1)} %fusion.85, f32[8,256]{1,0:T(8,128)S(1)} %gather_fusion.1), kind=kLoop, calls=%fused_computation.27.clone.1 | loop fusion | flops 36700160 | bytes 4202496 | tf_op jit(solution)/shard_map/while/body/eval_jaxpr/vmap()/div | solution.py:28
  500.5 5.9 %fusion.86 = f32[8,256,256]{2,1,0:T(8,128)S(1)} fusion(f32[8,256,256]{2,1,0:T(8,128)S(1)} %fusion.85, f32[8,256]{1,0:T(8,128)S(1)} %gather_fusion.1), kind=kLoop, calls=%fused_computation.27.clone.1 | loop fusion | flops 36700160 | bytes 4202496 | tf_op jit(solution)/shard_map/while/body/eval_jaxpr/vmap()/div | solution.py:28
  (363 shorter events, 124.6 us)
Async XLA Ops:
  0.0 29.6 %copy-start = (f32[64,3,256]{2,0,1:T(8,128)S(1)}, f32[64,3,256]{2,0,1:T(8,128)}, u32[]{:S(2)}) copy-start(f32[64,3,256]{2,0,1:T(8,128)} %param.15) | copy-start | bytes 589828
  24.4 8.3 %all-to-all-start = ((s32[4,8,8]{2,1,0:T(8,128)}), s32[4,8,8]{2,1,0:T(8,128)S(1)}, u32[]{:S(2)}, u32[]{:S(2)}) async-start(s32[4,8,8]{2,1,0:T(8,128)} %get-tuple-element.261), calls=%async_computation | async-start | bytes 32768 | tf_op jit(solution)/shard_map/all_to_all | solution.py:133
  29.6 3.0 copy-start.4
  32.7 7.1 %all-to-all-start.1 = ((s32[4,8,8]{2,1,0:T(8,128)}), s32[4,8,8]{2,1,0:T(8,128)S(1)}, u32[]{:S(2)}, u32[]{:S(2)}) async-start(s32[4,8,8]{2,1,0:T(8,128)} %get-tuple-element.260), calls=%async_computation.1 | async-start | bytes 32768 | tf_op jit(solution)/shard_map/all_to_all | solution.py:132
  39.8 15.1 %all-to-all-start.2 = ((f32[4,8,8,3,256]{4,2,1,3,0:T(8,128)}), f32[4,8,8,3,256]{4,2,1,3,0:T(8,128)S(1)}, u32[]{:S(2)}, u32[]{:S(2)}) async-start(f32[4,8,8,3,256]{4,2,1,3,0:T(8,128)} %copy_select_fusion), calls=%async_computation.2 | async-start | bytes 1572864 | tf_op jit(solution)/shard_map/all_to_all | solution.py:131
  54.9 12.3 %all-to-all-start.4 = ((s32[8,1,16]{2,1,0:T(1,128)}), s32[8,1,16]{2,1,0:T(1,128)S(1)}, u32[]{:S(2)}, u32[]{:S(2)}) async-start(s32[8,1,16]{2,1,0:T(1,128)} %bitcast.40), calls=%async_computation.4 | async-start | bytes 8192 | tf_op jit(solution)/shard_map/all_to_all | solution.py:149
  60.7 9.9 %copy-start.3 = (f32[3,4096]{1,0:T(4,128)S(1)}, f32[3,4096]{1,0:T(4,128)}, u32[]{:S(2)}) copy-start(f32[3,4096]{1,0:T(4,128)} %param.20) | copy-start | bytes 147460
  67.1 173.5 %all-to-all-start.3 = ((f32[8,16,3,256]{3,1,2,0:T(8,128)}), f32[8,16,3,256]{3,1,2,0:T(8,128)S(1)}, u32[]{:S(2)}, u32[]{:S(2)}) async-start(f32[8,16,3,256]{3,1,2,0:T(8,128)} %copy_select_fusion.1), calls=%async_computation.3 | async-start | bytes 786432 | tf_op jit(solution)/shard_map/all_to_all | solution.py:148
  139.0 5.4 %copy-start.6 = (f32[4096]{0:T(1024)S(1)}, f32[4096]{0:T(1024)}, u32[]{:S(2)}) copy-start(f32[4096]{0:T(1024)} %param.21) | copy-start | bytes 49156
  149.8 90.6 %copy-start.7 = (s32[64]{0:T(128)S(1)}, s32[64]{0:T(128)}, u32[]{:S(2)}) copy-start(s32[64]{0:T(128)} %param.23) | copy-start | bytes 772
  401.3 7.9 %copy-start.8 = (s32[64]{0:T(128)S(1)}, s32[64]{0:T(128)}, u32[]{:S(2)}) copy-start(s32[64]{0:T(128)} %param.17) | copy-start | bytes 772
  403.2 18.1 %all-to-all-start.5 = ((f32[8,16,3,256]{3,1,2,0:T(8,128)}), f32[8,16,3,256]{3,1,2,0:T(8,128)S(1)}, u32[]{:S(2)}, u32[]{:S(2)}) async-start(f32[8,16,3,256]{3,1,2,0:T(8,128)} %copy.114), calls=%async_computation.5 | async-start | bytes 786432 | tf_op jit(solution)/shard_map/all_to_all | solution.py:160
  424.1 84.4 %all-to-all-start.6 = ((f32[4,8,8,3,256]{4,2,3,1,0:T(8,128)}), f32[4,8,8,3,256]{4,2,3,1,0:T(8,128)S(1)}, u32[]{:S(2)}, u32[]{:S(2)}) async-start(f32[4,8,8,3,256]{4,2,3,1,0:T(8,128)} %copy.118), calls=%async_computation.6 | async-start | bytes 1572864 | tf_op jit(solution)/shard_map/all_to_all | solution.py:165
  427.6 80.8 %copy-start.5 = (s32[64,256]{1,0:T(8,128)S(1)}, s32[64,256]{1,0:T(8,128)}, u32[]{:S(2)}) copy-start(s32[64,256]{1,0:T(8,128)} %param.16) | copy-start | bytes 196612
  427.6 0.7 copy-start.1
  436.0 1.7 copy-start.2
  437.7 0.7 copy-start.1
  446.0 1.7 copy-start.2
  447.7 0.7 copy-start.1
  456.1 1.7 copy-start.2
  457.8 0.7 copy-start.1
  466.1 1.7 copy-start.2
  467.9 0.7 copy-start.1
  476.2 1.7 copy-start.2
  477.9 0.7 copy-start.1
  486.2 1.7 copy-start.2
  488.0 0.7 copy-start.1
  496.3 1.7 copy-start.2
  498.0 0.7 copy-start.1
  506.4 1.7 copy-start.2
